TPU v7x, 64 devices: a 2x2x8 block of a 4x4x8 slice. The times are simulated.
64 devices in a mesh: rep: 4 (over x, y), dp: 16 (over z, core).
Axes of the slice: x: 2, y: 2, z: 8, core: 2. Of those that a mesh axis runs over, the one named last changes fastest.
The devices are a block of a 4x4x8 slice.
Arguments:
- g_w_gate: bfloat16 [64, 2, 640, 3456], P(('rep', 'dp')), parts along dimension 0
- g_w_up: bfloat16 [64, 2, 640, 3456], P(('rep', 'dp')), parts along dimension 0
- g_w_down: bfloat16 [64, 2, 3456, 640], P(('rep', 'dp')), parts along dimension 0
- w_gate: bfloat16 [2, 640, 3456], replicated
- w_up: bfloat16 [2, 640, 3456], replicated
- w_down: bfloat16 [2, 3456, 640], replicated
- m_w_gate: float32 [2, 640, 3456], P(None, 'dp')
- m_w_up: float32 [2, 640, 3456], P(None, 'dp')
- m_w_down: float32 [2, 3456, 640], P(None, 'dp')
- v_w_gate: float32 [2, 640, 3456], P(None, 'dp')
- v_w_up: float32 [2, 640, 3456], P(None, 'dp')
- v_w_down: float32 [2, 3456, 640], P(None, 'dp')
Outputs:
- output 1: bfloat16 [8, 640, 3456], P('rep'), parts along dimension 0
- output 2: bfloat16 [8, 640, 3456], P('rep'), parts along dimension 0
- output 3: bfloat16 [8, 3456, 640], P('rep'), parts along dimension 0
- output 4: float32 [8, 640, 3456], P('rep', 'dp'), parts along dimension 0
- output 5: float32 [8, 640, 3456], P('rep', 'dp'), parts along dimension 0
- output 6: float32 [8, 3456, 640], P('rep', 'dp'), parts along dimension 0
- output 7: float32 [8, 640, 3456], P('rep', 'dp'), parts along dimension 0
- output 8: float32 [8, 640, 3456], P('rep', 'dp'), parts along dimension 0
- output 9: float32 [8, 3456, 640], P('rep', 'dp'), parts along dimension 0
There are 4 independent parts. A program takes and returns all parts, laid end to end along the dimension named above; an argument that names none is the same for every part.
All inputs are finite; a program needn't handle non-finite values.
Results may differ from a plain program's by a relative error of at most 0.022.
Values are sent between devices in bfloat16 or wider.
A program may use at most 768 MiB of HBM per device.

v0:
```python
import jax
import jax.numpy as jnp
from jax import lax
from jax.sharding import PartitionSpec as P


def adamw(w, m, v, g):
    m = 0.9 * m + 0.1 * g
    v = 0.95 * v + 0.05 * g * g
    step = m * lax.rsqrt(v + 1e-8) + 0.1 * w
    return (w - 0.02 * step).astype(jnp.bfloat16), m, v


def solution(mesh):
    def step(*arrays):
        terms, weights, m, v = (arrays[i : i + 3] for i in (0, 3, 6, 9))
        gradients = [lax.psum_scatter(t[0], "dp", scatter_dimension=1, tiled=True).astype(jnp.float32) for t in terms]
        me = lax.axis_index("dp")
        own = [lax.dynamic_slice_in_dim(w, me * one.shape[1], one.shape[1], 1).astype(jnp.float32) for w, one in zip(weights, m, strict=True)]
        new = [adamw(w, m, v, g) for w, m, v, g in zip(own, m, v, gradients, strict=True)]
        whole = [lax.all_gather(one[0], "dp", axis=1, tiled=True) for one in new]
        return (*whole, *(one[1] for one in new), *(one[2] for one in new))

    all_of, cut = P(None, None, None), P(None, "dp", None)
    return jax.shard_map(
        step,
        mesh=mesh,
        in_specs=(P(("rep", "dp"), None, None, None),) * 3 + (all_of,) * 3 + (cut,) * 6,
        out_specs=(P("rep", None, None),) * 3 + (P("rep", "dp", None),) * 6,
        check_vma=False,
    )
```

profile of v0, /device:TPU:21, one launch (start us, length us, event | category | flops | bytes accessed | tf_op | source)
XLA Modules:
  0.0 459.7 jit_solution(15978662882482003849)
XLA Ops:
  7.3 34.0 %copy.21 = bf16[2,640,3456]{2,0,1:T(2,128)(2,1)} copy(bf16[2,640,3456]{2,1,0:T(8,128)(2,1)} %bitcast.21) | data formatting | bytes 17694720
  41.3 8.5 %copy.27 = bf16[80,8,2,3456]{3,1,2,0:T(8,128)(2,1)} copy(bf16[80,8,2,3456]{3,2,1,0:T(2,128)(2,1)} %bitcast.18) | data formatting | bytes 17694720
  49.8 0.1 reduce-scatter.12.cloned.1.call-start
  49.9 34.0 %copy.23 = bf16[2,640,3456]{2,0,1:T(2,128)(2,1)} copy(bf16[2,640,3456]{2,1,0:T(8,128)(2,1)} %bitcast.22) | data formatting | bytes 17694720
  83.9 8.5 %copy.28 = bf16[80,8,2,3456]{3,1,2,0:T(8,128)(2,1)} copy(bf16[80,8,2,3456]{3,2,1,0:T(2,128)(2,1)} %bitcast.19) | data formatting | bytes 17694720
  92.4 0.1 reduce-scatter.14.cloned.1.call-start
  92.5 41.6 %copy.25 = bf16[2,3456,640]{2,0,1:T(2,128)(2,1)} copy(bf16[2,3456,640]{2,1,0:T(8,128)(2,1)} %bitcast.23) | data formatting | bytes 17694720
  134.1 8.5 %copy.29 = bf16[432,8,2,640]{3,1,2,0:T(8,128)(2,1)} copy(bf16[432,8,2,640]{3,2,1,0:T(2,128)(2,1)} %bitcast.20) | data formatting | bytes 17694720
  142.6 0.2 all-gather.4.cloned.1.call-start
  142.9 1.4 reshape.19
  144.3 2.9 fusion.2
  147.3 43.3 %reduce-scatter.12.cloned.1.call-done = bf16[40,6912]{1,0:T(8,128)(2,1)} async-done(((bf16[640,6912]{1,0:T(8,128)(2,1)}), bf16[40,6912]{1,0:T(8,128)(2,1)}) %reduce-scatter.12.cloned.1.call-update) | async-done | bytes 552976
  190.6 1.2 reshape.21
  191.9 3.3 fusion.6
  195.2 0.1 all-gather.8.cloned.1.call-start
  195.3 65.2 %reduce-scatter.14.cloned.1.call-done = bf16[216,1280]{1,0:T(8,128)(2,1)} async-done(((bf16[3456,1280]{1,0:T(8,128)(2,1)}), bf16[216,1280]{1,0:T(8,128)(2,1)}) %reduce-scatter.14.cloned.1.call-update) | async-done | bytes 552976
  260.4 1.8 reshape.23
  262.2 2.9 fusion.10
  265.2 54.0 %all-gather.4.cloned.1.call-done = bf16[2,640,3456]{2,1,0:T(8,128)(2,1)} async-done(((bf16[2,40,3456]{2,1,0:T(8,128)(2,1)}), bf16[2,640,3456]{2,1,0:T(8,128)(2,1)}) %all-gather.4.cloned.1.call-update) | async-done | bytes 8847376 | tf_op jit(solution)/shard_map/all_gather | solution.py:21
  319.3 55.2 %all-gather.6.cloned.1.call-done = bf16[2,640,3456]{2,1,0:T(8,128)(2,1)} async-done(((bf16[2,40,3456]{2,1,0:T(8,128)(2,1)}), bf16[2,640,3456]{2,1,0:T(8,128)(2,1)}) %all-gather.6.cloned.1.call-update) | async-done | bytes 8847376 | tf_op jit(solution)/shard_map/all_gather | solution.py:21
  374.5 55.2 %all-gather.8.cloned.1.call-done = bf16[2,3456,640]{2,1,0:T(8,128)(2,1)} async-done(((bf16[2,216,640]{2,1,0:T(8,128)(2,1)}), bf16[2,3456,640]{2,1,0:T(8,128)(2,1)}) %all-gather.8.cloned.1.call-update) | async-done | bytes 8847376 | tf_op jit(solution)/shard_map/all_gather | solution.py:21
  429.7 7.7 %copy.45 = bf16[2,640,3456]{2,1,0:T(8,128)(2,1)} copy(bf16[2,640,3456]{2,1,0:T(8,128)(2,1)} %all-gather.4.cloned.1.call-done) | data formatting | bytes 17694720
  437.4 7.7 %copy.46 = bf16[2,640,3456]{2,1,0:T(8,128)(2,1)} copy(bf16[2,640,3456]{2,1,0:T(8,128)(2,1)} %all-gather.6.cloned.1.call-done) | data formatting | bytes 17694720
  445.1 7.8 %copy.47 = bf16[2,3456,640]{2,1,0:T(8,128)(2,1)} copy(bf16[2,3456,640]{2,1,0:T(8,128)(2,1)} %all-gather.8.cloned.1.call-done) | data formatting | bytes 17694720
  (19 shorter events, 0.5 us)
Async XLA Ops:
  7.2 135.7 %reduce-scatter.10.cloned.1.call-start = ((), (), s32[]{:S(2)}) async-start(), calls=%async_computation.6 | async-start | bytes 9400320
  49.8 140.8 %reduce-scatter.12.cloned.1.call-start = ((), (), s32[]{:S(2)}) async-start(), calls=%async_computation.7 | async-start | bytes 9400320
  92.4 168.0 %reduce-scatter.14.cloned.1.call-start = ((), (), s32[]{:S(2)}) async-start(), calls=%async_computation.8 | async-start | bytes 9400320
  142.5 1.7 copy-start.1
  142.6 1.7 copy-start
  142.6 176.6 %all-gather.4.cloned.1.call-start = ((), (), s32[]{:S(2)}) async-start(), calls=%async_computation.3 | async-start | bytes 9400320 | tf_op jit(solution)/shard_map/all_gather | solution.py:21
  147.2 44.7 %copy-start.2 = (f32[2,40,3456]{2,1,0:T(8,128)S(1)}, f32[2,40,3456]{2,1,0:T(8,128)}, u32[]{:S(2)}) copy-start(f32[2,40,3456]{2,1,0:T(8,128)} %param.22) | copy-start | bytes 3317764
  147.2 227.3 %all-gather.6.cloned.1.call-start = ((), (), s32[]{:S(2)}) async-start(), calls=%async_computation.4 | async-start | bytes 9400320 | tf_op jit(solution)/shard_map/all_gather | solution.py:21
  191.8 70.4 %copy-start.4 = (f32[2,216,640]{2,1,0:T(8,128)S(1)}, f32[2,216,640]{2,1,0:T(8,128)}, u32[]{:S(2)}) copy-start(f32[2,216,640]{2,1,0:T(8,128)} %param.20) | copy-start | bytes 3317764
  195.2 67.1 %copy-start.3 = (f32[2,216,640]{2,1,0:T(8,128)S(1)}, f32[2,216,640]{2,1,0:T(8,128)}, u32[]{:S(2)}) copy-start(f32[2,216,640]{2,1,0:T(8,128)} %param.23) | copy-start | bytes 3317764
  195.2 234.5 %all-gather.8.cloned.1.call-start = ((), (), s32[]{:S(2)}) async-start(), calls=%async_computation.5 | async-start | bytes 9400320 | tf_op jit(solution)/shard_map/all_gather | solution.py:21
Sparse Core Ops, SparseCore 0:
  49.9 70.2 reduce-scatter.9
  123.1 67.4 reduce-scatter.11
  193.0 67.3 reduce-scatter.13
  262.5 56.7 all-gather.3
  321.3 53.1 all-gather.5
  376.5 53.1 all-gather.7
where the time goes:
time: 460 us
  waiting for transfers between devices  273 us (59%)
  local copies, waits for them, and re-layouts  163 us (35%)
  between operations  14.2 us (3%)
  other arithmetic  9.09 us (2%)
    all_gather x3, waiting for transfers between devices, step(): whole = [lax.all_gather(one[0], 'dp', axis=1, tiled=True) for one in new]  165 us
    unnamed x22, local copies, waits for them, and re-layouts  163 us
    unnamed x9, waiting for transfers between devices  109 us
  transfers between devices with their start and end apart: 6, of which 5 were waited for; matrix products, arithmetic and copies ran while one was open for 23% of the time, Pallas kernels for 0%

commit v1 on v0

v1 whole, which is shorter than its diff:
```python
import functools

import jax
import jax.numpy as jnp
from jax import lax
from jax.experimental import pallas as pl
from jax.experimental.pallas import tpu as pltpu
from jax.sharding import PartitionSpec as P

MESH = pl.DeviceIdType.MESH
F32 = jnp.float32
BF16 = jnp.bfloat16
TILE = 8


def adamw(w, m, v, g):
    m = 0.9 * m + 0.1 * g
    v = 0.95 * v + 0.05 * g * g
    step = m * lax.rsqrt(v + 1e-8) + 0.1 * w
    return (w - 0.02 * step).astype(BF16), m, v


def rows_loop(rows, cols, body):
    step = TILE
    while rows % (2 * step) == 0 and 2 * step * cols <= 32 * 1024:
        step *= 2
    while rows % (3 * step) == 0 and 3 * step * cols <= 32 * 1024:
        step *= 3

    def one(i, carry):
        body(pl.ds(pl.multiple_of(i * step, TILE), step))
        return carry

    lax.fori_loop(0, rows // step, one, 0)


def kernel(n, *refs):
    g, w, m_in, v_in, w_out, m_out, v_out = (refs[i : i + 3] for i in range(0, 21, 3))
    own, term, run = (refs[i : i + 3] for i in range(21, 30, 3))
    own_sem, mom_sem, term_send, term_recv, rs_send, rs_recv, ag_send, ag_recv, fw_send, fw_recv = refs[30:]
    chips = n // 2
    me = lax.axis_index("dp")
    z, core = me // 2, lax.rem(me, 2)
    partner = me + 1 - 2 * core
    sign = (1, -1)
    ahead = [lax.rem(me + 2 * sign[d] + n, n) for d in range(2)]
    chunks = [(k, d) for k in range(3) for d in range(2)]

    def rs_block(d, s):
        return lax.rem(z - sign[d] * (s + 1) + 2 * chips, chips)

    def ag_block(d, t):
        return lax.rem(z - sign[d] * t + chips, chips)

    def own_copy(k, d, s):
        return pltpu.make_async_copy(g[k].at[d, 2 * rs_block(d, s) + core], own[k].at[d, lax.rem(s, 2)], own_sem.at[d, lax.rem(s, 2), k])

    def remote(src, dst, send, recv, to):
        return pltpu.make_async_remote_copy(src_ref=src, dst_ref=dst, send_sem=send, recv_sem=recv, device_id={"dp": to}, device_id_type=MESH)

    def term_copy(k, d, s):
        src = g[k].at[d, 2 * rs_block(d, s) + 1 - core]
        return remote(src, term[k].at[d, s], term_send.at[d, lax.rem(s, 2), k], term_recv.at[d, s, k], partner)

    def rs_copy(k, d, s):
        return remote(term[k].at[d, s], run[k].at[d, s], rs_send.at[d, lax.rem(s, 2), k], rs_recv.at[d, s, k], ahead[d])

    def ag_copy(k, d, t):
        at = w_out[k].at[d, 2 * ag_block(d, t) + core]
        return remote(at, at, ag_send.at[d, lax.rem(t, 2), k], ag_recv.at[d, t, k], ahead[d])

    def ag_arrival(k, d, t):
        at = w_out[k].at[d, 2 * ag_block(d, t + 1) + core]
        return remote(at, at, ag_send.at[d, lax.rem(t, 2), k], ag_recv.at[d, t, k], ahead[d])

    def fw_copy(k, d, t, whose):
        at = w_out[k].at[d, 2 * ag_block(d, t) + whose]
        return remote(at, at, fw_send.at[d, lax.rem(t, 2), k], fw_recv.at[d, t, k], partner)

    def mom_copies(k, d):
        return (
            pltpu.make_async_copy(m_in[k].at[d], m_out[k].at[d], mom_sem.at[0, d, k]),
            pltpu.make_async_copy(v_in[k].at[d], v_out[k].at[d], mom_sem.at[1, d, k]),
            pltpu.make_async_copy(w[k].at[d, me], w_out[k].at[d, me], mom_sem.at[2, d, k]),
        )

    for k, d in chunks:
        own_copy(k, d, 0).start()

    barrier = pltpu.get_barrier_semaphore()
    for peer in (partner, *ahead):
        pl.semaphore_signal(barrier, inc=1, device_id={"dp": peer}, device_id_type=MESH)
    pl.semaphore_wait(barrier, 3)

    for k, d in chunks:
        term_copy(k, d, 0).start()

    def scatter_step(s, first):
        for k, d in chunks:
            own_copy(k, d, s).wait()
            term_copy(k, d, s).wait_recv()
            if not first:
                rs_copy(k, d, s - 1).wait_recv()
            mine, other, sums = own[k].at[d, lax.rem(s, 2)], term[k].at[d, s], run[k].at[d, s - 1]

            def add(at):
                total = mine[at, :].astype(F32) + other[at, :].astype(F32)
                if not first:
                    total += sums[at, :].astype(F32)
                other[at, :] = total.astype(BF16)

            rows_loop(mine.shape[0], mine.shape[1], add)
            own_copy(k, d, s + 1).start()
            if not first:
                term_copy(k, d, s - 1).wait_send()
            term_copy(k, d, s + 1).start()
            if first:
                for copy in mom_copies(k, d):
                    copy.start()
            if not first:

                @pl.when(s >= 2)
                def _():
                    rs_copy(k, d, s - 2).wait_send()

            rs_copy(k, d, s).start()

    scatter_step(0, True)
    lax.fori_loop(1, chips - 1, lambda s, c: (scatter_step(s, False), c)[1], 0)

    last = chips - 1
    for k, d in chunks:
        own_copy(k, d, last).wait()
        term_copy(k, d, last).wait_recv()
        rs_copy(k, d, last - 1).wait_recv()
        for copy in mom_copies(k, d):
            copy.wait()
        mine, other, sums = own[k].at[d, last % 2], term[k].at[d, last], run[k].at[d, last - 1]
        mo, vo, wo = m_out[k].at[d], v_out[k].at[d], w_out[k].at[d, me]

        def update(at):
            total = mine[at, :].astype(F32) + other[at, :].astype(F32) + sums[at, :].astype(F32)
            grad = total.astype(BF16).astype(F32)
            new_w, new_m, new_v = adamw(wo[at, :].astype(F32), mo[at, :], vo[at, :], grad)
            mo[at, :] = new_m
            vo[at, :] = new_v
            wo[at, :] = new_w

        rows_loop(mine.shape[0], mine.shape[1], update)
        term_copy(k, d, last - 1).wait_send()
        term_copy(k, d, last).wait_send()
        ag_copy(k, d, 0).start()
        fw_copy(k, d, 0, core).start()
        rs_copy(k, d, last - 2).wait_send()

    def gather_step(t, c):
        for k, d in chunks:
            ag_arrival(k, d, t - 1).wait_recv()

            @pl.when(t >= 2)
            def _():
                ag_copy(k, d, t - 2).wait_send()
                fw_copy(k, d, t - 2, core).wait_send()

            ag_copy(k, d, t).start()
            fw_copy(k, d, t, core).start()
        return c

    lax.fori_loop(1, chips - 1, gather_step, 0)
    for k, d in chunks:
        ag_arrival(k, d, last - 1).wait_recv()
        fw_copy(k, d, last - 2, core).wait_send()
        fw_copy(k, d, last, core).start()
    for k, d in chunks:
        rs_copy(k, d, last - 1).wait_send()
        ag_copy(k, d, last - 2).wait_send()
        ag_copy(k, d, last - 1).wait_send()
        fw_copy(k, d, last - 1, core).wait_send()
        fw_copy(k, d, last, core).wait_send()

    def landed(t, c):
        for k, d in chunks:
            fw_copy(k, d, t, 1 - core).wait_recv()
        return c

    lax.fori_loop(0, chips, landed, 0)


def write_out(*refs):
    count = len(refs) // 2
    copies = []
    for i in range(count):
        for j in range(refs[i].shape[0]):
            copies.append(pltpu.make_async_copy(refs[i].at[j], refs[count + i].at[j], refs[-1].at[i, j]))
    for copy in copies:
        copy.start()
    for copy in copies:
        copy.wait()


def solution(mesh):
    n = mesh.shape["dp"]
    chips = n // 2

    def step(*arrays):
        terms, weights, m, v = (arrays[i : i + 3] for i in (0, 3, 6, 9))
        layers = m[0].shape[0]
        blocks = [(one.shape[1], one.shape[2]) for one in m]
        terms = [t.reshape(layers, n, *b) for t, b in zip(terms, blocks, strict=True)]
        weights = [w.reshape(layers, n, *b) for w, b in zip(weights, blocks, strict=True)]
        dma = pltpu.SemaphoreType.DMA
        out = pl.pallas_call(
            functools.partial(kernel, n),
            out_shape=[pltpu.VMEM((layers, n, *b), BF16) for b in blocks] + [pltpu.VMEM((layers, *b), F32) for b in blocks] * 2,
            in_specs=[pl.BlockSpec(memory_space=pltpu.HBM)] * 12,
            out_specs=[pl.BlockSpec(memory_space=pltpu.VMEM)] * 9,
            scratch_shapes=[
                *(pltpu.VMEM((layers, 2, *b), BF16) for b in blocks),
                *(pltpu.VMEM((layers, chips, *b), BF16) for b in blocks),
                *(pltpu.VMEM((layers, chips - 1, *b), BF16) for b in blocks),
                dma((layers, 2, 3)),
                dma((3, layers, 3)),
                dma((layers, 2, 3)),
                dma((layers, chips, 3)),
                dma((layers, 2, 3)),
                dma((layers, chips - 1, 3)),
                dma((layers, 2, 3)),
                dma((layers, chips - 1, 3)),
                dma((layers, 2, 3)),
                dma((layers, chips, 3)),
            ],
            compiler_params=pltpu.CompilerParams(collective_id=0, has_side_effects=True, vmem_limit_bytes=28 * 1024 * 1024),
        )(*terms, *weights, *m, *v)
        out = [pl.pallas_call(
            write_out,
            out_shape=[pltpu.HBM(o.shape, o.dtype) for o in part],
            in_specs=[pl.BlockSpec(memory_space=pltpu.VMEM)] * len(part),
            out_specs=[pl.BlockSpec(memory_space=pltpu.HBM)] * len(part),
            scratch_shapes=[dma((9, layers))],
            compiler_params=pltpu.CompilerParams(vmem_limit_bytes=1024 * 1024),
        )(*part) for part in (out[:3], out[3:])]
        out = [x for p in out for x in p]
        whole = [one.reshape(layers, n * b[0], b[1]) for one, b in zip(out[:3], blocks, strict=True)]
        return (*whole, *out[3:])

    all_of, cut = P(None, None, None), P(None, "dp", None)
    return jax.shard_map(
        step,
        mesh=mesh,
        in_specs=(P(("rep", "dp"), None, None, None),) * 3 + (all_of,) * 3 + (cut,) * 6,
        out_specs=(P("rep", None, None),) * 3 + (P("rep", "dp", None),) * 6,
        check_vma=False,
    )
```

time: 460 us -> 277 us (0.60)
  Pallas kernels: 0 us -> 276 us
  waiting for transfers between devices: 273 us -> 0 us
  local copies, waits for them, and re-layouts: 163 us -> 0 us
  between operations: 14.2 us -> 0.66 us
  other arithmetic: 9.09 us -> 0 us
    pallas_call x0 -> x3, Pallas kernels: none -> 276 us  [the longest x1 264 us: step(): pl.pallas_call(functools.partial(kernel, n), out_shape=[pltpu.VMEM((layer...]
    all_gather x3 -> x0, waiting for transfers between devices: 165 us -> none  [step(): whole = [lax.all_gather(one[0], 'dp', axis=1, tiled=True) for one in new]]
    unnamed x22 -> x0, local copies, waits for them, and re-layouts: 163 us -> none
    unnamed x9 -> x0, waiting for transfers between devices: 109 us -> none
    convert_element_type x3 -> x0, other arithmetic: 9.09 us -> none  [adamw(): return ((w - 0.02 * step).astype(jnp.bfloat16), m, v)]
  transfers between devices with their start and end apart: 6 -> 0, of which waited for: 5 -> 0; matrix products, arithmetic and copies ran while one was open for 23% -> 0% of each run, Pallas kernels for 0% -> 0%
where the time goes in v1:
time: 277 us
  Pallas kernels  276 us (100%)
    pallas_call x1, Pallas kernels, step(): pl.pallas_call(functools.partial(kernel, n), out_shape=[pltpu.VMEM((layer...  264 us
    pallas_call x2, Pallas kernels, step(): pl.pallas_call(write_out, out_shape=[pltpu.HBM(o.shape, o.dtype) for o in...  11.9 us

profile of v1, /device:TPU:21, one launch (start us, length us, event | category | flops | bytes accessed | tf_op | source)
XLA Modules:
  0.0 277.1 jit_solution(8076146778197273554)
XLA Ops:
  0.6 264.5 %shard_map.187 = (bf16[2,16,40,3456]{3,2,1,0:T(8,128)(2,1)S(1)}, bf16[2,16,40,3456]{3,2,1,0:T(8,128)(2,1)S(1)}, bf16[2,16,216,640]{3,2,1,0:T(8,128)(2,1)S(1)}, f...) custom-call(bf16[2,16,40,3456]{3,2,1,0:T(8,128)(2,1)} %bitcast.9, ...), custom_call_target="tpu_custom_call" | custom-call | tf_op jit(solution)/shard_map/pallas_call | solution.py:212
  265.1 9.0 %shard_map.188 = (bf16[2,16,40,3456]{3,2,1,0:T(8,128)(2,1)}, bf16[2,16,40,3456]{3,2,1,0:T(8,128)(2,1)}, bf16[2,16,216,640]{3,2,1,0:T(8,128)(2,1)}) custom-call(bf16[2,16,40,3456]{3,2,1,0:T(8,128)(2,1)S(1)} %get-tuple-element.27.refs_0_, bf16[2,16,40,3456]{3,2,1,0:T(8,128)(2,1)S(1)} %get-tuple-element.28.refs_1_, ...), custom_call_target="tpu_custom_call" | custom-call | tf_op jit(solution)/shard_map/pallas_call | solution.py:234
  274.2 2.9 %shard_map.189 = (f32[2,40,3456]{2,1,0:T(8,128)}, f32[2,40,3456]{2,1,0:T(8,128)}, f32[2,216,640]{2,1,0:T(8,128)}, f32[2,40,3456]{2,1,0:T(8,128)}, f32[2,40,3456]{2,1,0:T(8,128)}, /*index=5*/f32[2,216,640]{2,1,0:T(8,128)}) custom-call(f32[2,40,3456]{2,1,0:T(8,128)S(1)} %get-tuple-element.33.refs_0_, f32[2,40,3456]{2,1,0:T(8,128)S(1)} %get-tuple-element.34.refs_1_, ...), custom_call_target="tpu_custom_call" | custom-call | tf_op jit(solution)/shard_map/pallas_call | solution.py:234

commit v2 on v1

v2 whole, which is shorter than its diff:
```python
import functools

import jax
import jax.numpy as jnp
from jax import lax
from jax.experimental import pallas as pl
from jax.experimental.pallas import tpu as pltpu
from jax.sharding import PartitionSpec as P

MESH = pl.DeviceIdType.MESH
F32 = jnp.float32
BF16 = jnp.bfloat16
TILE = 8


def adamw(w, m, v, g):
    m = 0.9 * m + 0.1 * g
    v = 0.95 * v + 0.05 * g * g
    step = m * lax.rsqrt(v + 1e-8) + 0.1 * w
    return (w - 0.02 * step).astype(BF16), m, v


def units_of(blocks):
    units = []
    for k, (rows, cols) in enumerate(blocks):
        short = TILE * max(1, 8 * 3456 // (TILE * cols))
        if k == 0:
            units += [(k, 0, short), (k, short, rows - short)]
        elif k == len(blocks) - 1:
            units += [(k, 0, rows - short), (k, rows - short, short)]
        else:
            units.append((k, 0, rows))
    return units


def rows_loop(first, rows, cols, body):
    step = TILE
    while rows % (2 * step) == 0 and 2 * step * cols <= 32 * 1024:
        step *= 2
    while rows % (3 * step) == 0 and 3 * step * cols <= 32 * 1024:
        step *= 3

    def one(i, carry):
        body(pl.ds(pl.multiple_of(first + i * step, TILE), step))
        return carry

    lax.fori_loop(0, rows // step, one, 0)


def kernel(n, *refs):
    g, w, m_in, v_in, w_out, m_out, v_out = (refs[i : i + 3] for i in range(0, 21, 3))
    own, term, run = (refs[i : i + 3] for i in range(21, 30, 3))
    own_sem, mom_sem, term_send, term_recv, rs_send, rs_recv, ag_send, ag_recv, fw_send, fw_recv = refs[30:]
    chips = n // 2
    me = lax.axis_index("dp")
    z, core = me // 2, lax.rem(me, 2)
    partner = me + 1 - 2 * core
    sign = (1, -1)
    ahead = [lax.rem(me + 2 * sign[d] + n, n) for d in range(2)]
    units = units_of([one.shape[1:] for one in m_in])
    chunks = [(u, d) for u in range(len(units)) for d in range(2)]

    def part(refs, u, *at):
        k, first, rows = units[u]
        return refs[k].at[(*at, pl.ds(first, rows))]

    def rs_block(d, s):
        return lax.rem(z - sign[d] * (s + 1) + 2 * chips, chips)

    def ag_block(d, t):
        return lax.rem(z - sign[d] * t + chips, chips)

    def own_copy(u, d, s):
        at = lax.rem(s, 2)
        return pltpu.make_async_copy(part(g, u, d, 2 * rs_block(d, s) + core), part(own, u, d, at), own_sem.at[d, at, u])

    def remote(src, dst, send, recv, to):
        return pltpu.make_async_remote_copy(src_ref=src, dst_ref=dst, send_sem=send, recv_sem=recv, device_id={"dp": to}, device_id_type=MESH)

    def term_copy(u, d, s):
        src = part(g, u, d, 2 * rs_block(d, s) + 1 - core)
        return remote(src, part(term, u, d, s), term_send.at[d, lax.rem(s, 2), u], term_recv.at[d, s, u], partner)

    def rs_copy(u, d, s):
        return remote(part(term, u, d, s), part(run, u, d, s), rs_send.at[d, lax.rem(s, 2), u], rs_recv.at[d, s, u], ahead[d])

    def ag_copy(u, d, t, block=None):
        at = part(w_out, u, d, 2 * (ag_block(d, t) if block is None else block) + core)
        return remote(at, at, ag_send.at[d, lax.rem(t, 2), u], ag_recv.at[d, t, u], ahead[d])

    def ag_arrival(u, d, t):
        return ag_copy(u, d, t, ag_block(d, t + 1))

    def fw_copy(u, d, t, whose):
        at = part(w_out, u, d, 2 * ag_block(d, t) + whose)
        return remote(at, at, fw_send.at[d, lax.rem(t, 2), u], fw_recv.at[d, t, u], partner)

    def mom_copies(u, d):
        return (
            pltpu.make_async_copy(part(m_in, u, d), part(m_out, u, d), mom_sem.at[0, d, u]),
            pltpu.make_async_copy(part(v_in, u, d), part(v_out, u, d), mom_sem.at[1, d, u]),
            pltpu.make_async_copy(part(w, u, d, me), part(w_out, u, d, me), mom_sem.at[2, d, u]),
        )

    for u, d in chunks:
        own_copy(u, d, 0).start()

    barrier = pltpu.get_barrier_semaphore()
    for peer in (partner, *ahead):
        pl.semaphore_signal(barrier, inc=1, device_id={"dp": peer}, device_id_type=MESH)
    pl.semaphore_wait(barrier, 3)

    for u, d in chunks:
        term_copy(u, d, 0).start()

    def scatter_step(s, first):
        for u, d in chunks:
            k, row, rows = units[u]
            own_copy(u, d, s).wait()
            term_copy(u, d, s).wait_recv()
            if not first:
                rs_copy(u, d, s - 1).wait_recv()
            mine, other, sums = own[k].at[d, lax.rem(s, 2)], term[k].at[d, s], run[k].at[d, s - 1]

            def add(at):
                total = mine[at, :].astype(F32) + other[at, :].astype(F32)
                if not first:
                    total += sums[at, :].astype(F32)
                other[at, :] = total.astype(BF16)

            rows_loop(row, rows, mine.shape[1], add)
            own_copy(u, d, s + 1).start()
            if not first:
                term_copy(u, d, s - 1).wait_send()
            term_copy(u, d, s + 1).start()
            if not first:

                @pl.when(s >= 2)
                def _():
                    rs_copy(u, d, s - 2).wait_send()

            rs_copy(u, d, s).start()
            if first:
                for copy in mom_copies(u, d):
                    copy.start()

    scatter_step(0, True)
    lax.fori_loop(1, chips - 1, lambda s, c: (scatter_step(s, False), c)[1], 0)

    last = chips - 1
    for u, d in chunks:
        k, row, rows = units[u]
        own_copy(u, d, last).wait()
        term_copy(u, d, last).wait_recv()
        for copy in mom_copies(u, d):
            copy.wait()
        rs_copy(u, d, last - 1).wait_recv()
        mine, other, sums = own[k].at[d, last % 2], term[k].at[d, last], run[k].at[d, last - 1]
        mo, vo, wo = m_out[k].at[d], v_out[k].at[d], w_out[k].at[d, me]

        def update(at):
            total = mine[at, :].astype(F32) + other[at, :].astype(F32) + sums[at, :].astype(F32)
            grad = total.astype(BF16).astype(F32)
            new_w, new_m, new_v = adamw(wo[at, :].astype(F32), mo[at, :], vo[at, :], grad)
            mo[at, :] = new_m
            vo[at, :] = new_v
            wo[at, :] = new_w

        rows_loop(row, rows, mine.shape[1], update)
        term_copy(u, d, last - 1).wait_send()
        term_copy(u, d, last).wait_send()
        ag_copy(u, d, 0).start()
        fw_copy(u, d, 0, core).start()
        rs_copy(u, d, last - 2).wait_send()

    def gather_step(t, c):
        for u, d in chunks:
            ag_arrival(u, d, t - 1).wait_recv()

            @pl.when(t >= 2)
            def _():
                ag_copy(u, d, t - 2).wait_send()
                fw_copy(u, d, t - 2, core).wait_send()

            ag_copy(u, d, t).start()
            fw_copy(u, d, t, core).start()
        return c

    lax.fori_loop(1, chips - 1, gather_step, 0)
    for u, d in chunks:
        ag_arrival(u, d, last - 1).wait_recv()
        fw_copy(u, d, last - 2, core).wait_send()
        fw_copy(u, d, last, core).start()
    for u, d in chunks:
        rs_copy(u, d, last - 1).wait_send()
        ag_copy(u, d, last - 2).wait_send()
        ag_copy(u, d, last - 1).wait_send()
        fw_copy(u, d, last - 1, core).wait_send()
        fw_copy(u, d, last, core).wait_send()

    def landed(t, c):
        for u, d in chunks:
            fw_copy(u, d, t, 1 - core).wait_recv()
        return c

    lax.fori_loop(0, chips, landed, 0)


def write_out(*refs):
    count = len(refs) // 2
    copies = []
    for i in range(count):
        for j in range(refs[i].shape[0]):
            copies.append(pltpu.make_async_copy(refs[i].at[j], refs[count + i].at[j], refs[-1].at[i, j]))
    for copy in copies:
        copy.start()
    for copy in copies:
        copy.wait()


def solution(mesh):
    n = mesh.shape["dp"]
    chips = n // 2

    def step(*arrays):
        terms, weights, m, v = (arrays[i : i + 3] for i in (0, 3, 6, 9))
        layers = m[0].shape[0]
        blocks = [(one.shape[1], one.shape[2]) for one in m]
        terms = [t.reshape(layers, n, *b) for t, b in zip(terms, blocks, strict=True)]
        weights = [w.reshape(layers, n, *b) for w, b in zip(weights, blocks, strict=True)]
        dma = pltpu.SemaphoreType.DMA
        count = len(units_of(blocks))
        out = pl.pallas_call(
            functools.partial(kernel, n),
            out_shape=[pltpu.VMEM((layers, n, *b), BF16) for b in blocks] + [pltpu.VMEM((layers, *b), F32) for b in blocks] * 2,
            in_specs=[pl.BlockSpec(memory_space=pltpu.HBM)] * 12,
            out_specs=[pl.BlockSpec(memory_space=pltpu.VMEM)] * 9,
            scratch_shapes=[
                *(pltpu.VMEM((layers, 2, *b), BF16) for b in blocks),
                *(pltpu.VMEM((layers, chips, *b), BF16) for b in blocks),
                *(pltpu.VMEM((layers, chips - 1, *b), BF16) for b in blocks),
                dma((layers, 2, count)),
                dma((3, layers, count)),
                dma((layers, 2, count)),
                dma((layers, chips, count)),
                dma((layers, 2, count)),
                dma((layers, chips - 1, count)),
                dma((layers, 2, count)),
                dma((layers, chips - 1, count)),
                dma((layers, 2, count)),
                dma((layers, chips, count)),
            ],
            compiler_params=pltpu.CompilerParams(collective_id=0, has_side_effects=True, vmem_limit_bytes=28 * 1024 * 1024),
        )(*terms, *weights, *m, *v)
        out = [pl.pallas_call(
            write_out,
            out_shape=[pltpu.HBM(o.shape, o.dtype) for o in part],
            in_specs=[pl.BlockSpec(memory_space=pltpu.VMEM)] * len(part),
            out_specs=[pl.BlockSpec(memory_space=pltpu.HBM)] * len(part),
            scratch_shapes=[dma((9, layers))],
            compiler_params=pltpu.CompilerParams(vmem_limit_bytes=1024 * 1024),
        )(*part) for part in (out[:3], out[3:])]
        out = [x for p in out for x in p]
        whole = [one.reshape(layers, n * b[0], b[1]) for one, b in zip(out[:3], blocks, strict=True)]
        return (*whole, *out[3:])

    all_of, cut = P(None, None, None), P(None, "dp", None)
    return jax.shard_map(
        step,
        mesh=mesh,
        in_specs=(P(("rep", "dp"), None, None, None),) * 3 + (all_of,) * 3 + (cut,) * 6,
        out_specs=(P("rep", None, None),) * 3 + (P("rep", "dp", None),) * 6,
        check_vma=False,
    )
```

time: 277 us -> 278 us (level)
  no operation moved by 1% of the time
where the time goes in v2:
time: 278 us
  Pallas kernels  277 us (100%)
    pallas_call x1, Pallas kernels, step(): pl.pallas_call(functools.partial(kernel, n), out_shape=[pltpu.VMEM((layer...  265 us
    pallas_call x2, Pallas kernels, step(): pl.pallas_call(write_out, out_shape=[pltpu.HBM(o.shape, o.dtype) for o in...  11.9 us

profile of v2, /device:TPU:21, one launch (start us, length us, event | category | flops | bytes accessed | tf_op | source)
XLA Modules:
  0.0 277.6 jit_solution(6248413179224841982)
XLA Ops:
  0.6 265.0 %shard_map.187 = (bf16[2,16,40,3456]{3,2,1,0:T(8,128)(2,1)S(1)}, bf16[2,16,40,3456]{3,2,1,0:T(8,128)(2,1)S(1)}, bf16[2,16,216,640]{3,2,1,0:T(8,128)(2,1)S(1)}, f...) custom-call(bf16[2,16,40,3456]{3,2,1,0:T(8,128)(2,1)} %bitcast.9, ...), custom_call_target="tpu_custom_call" | custom-call | tf_op jit(solution)/shard_map/pallas_call | solution.py:233
  265.6 9.0 %shard_map.188 = (bf16[2,16,40,3456]{3,2,1,0:T(8,128)(2,1)}, bf16[2,16,40,3456]{3,2,1,0:T(8,128)(2,1)}, bf16[2,16,216,640]{3,2,1,0:T(8,128)(2,1)}) custom-call(bf16[2,16,40,3456]{3,2,1,0:T(8,128)(2,1)S(1)} %get-tuple-element.27.refs_0_, bf16[2,16,40,3456]{3,2,1,0:T(8,128)(2,1)S(1)} %get-tuple-element.28.refs_1_, ...), custom_call_target="tpu_custom_call" | custom-call | tf_op jit(solution)/shard_map/pallas_call | solution.py:255
  274.7 2.9 %shard_map.189 = (f32[2,40,3456]{2,1,0:T(8,128)}, f32[2,40,3456]{2,1,0:T(8,128)}, f32[2,216,640]{2,1,0:T(8,128)}, f32[2,40,3456]{2,1,0:T(8,128)}, f32[2,40,3456]{2,1,0:T(8,128)}, /*index=5*/f32[2,216,640]{2,1,0:T(8,128)}) custom-call(f32[2,40,3456]{2,1,0:T(8,128)S(1)} %get-tuple-element.33.refs_0_, f32[2,40,3456]{2,1,0:T(8,128)S(1)} %get-tuple-element.34.refs_1_, ...), custom_call_target="tpu_custom_call" | custom-call | tf_op jit(solution)/shard_map/pallas_call | solution.py:255

commit v3 on v2

--- a/solution.py
+++ b/solution.py
@@ -23,11 +23,8 @@
 def units_of(blocks):
     units = []
     for k, (rows, cols) in enumerate(blocks):
-        short = TILE * max(1, 8 * 3456 // (TILE * cols))
         if k == 0:
-            units += [(k, 0, short), (k, short, rows - short)]
-        elif k == len(blocks) - 1:
-            units += [(k, 0, rows - short), (k, rows - short, short)]
+            units += [(k, 0, TILE), (k, TILE, rows - TILE)]
         else:
             units.append((k, 0, rows))
     return units
@@ -50,7 +47,7 @@
 def kernel(n, *refs):
     g, w, m_in, v_in, w_out, m_out, v_out = (refs[i : i + 3] for i in range(0, 21, 3))
     own, term, run = (refs[i : i + 3] for i in range(21, 30, 3))
-    own_sem, mom_sem, term_send, term_recv, rs_send, rs_recv, ag_send, ag_recv, fw_send, fw_recv = refs[30:]
+    own_sem, mom_sem, term_send, term_recv, rs_send, ag_send, ring_recv, fw_send, fw_recv = refs[30:]
     chips = n // 2
     me = lax.axis_index("dp")
     z, core = me // 2, lax.rem(me, 2)
@@ -79,28 +76,32 @@
 
     def term_copy(u, d, s):
         src = part(g, u, d, 2 * rs_block(d, s) + 1 - core)
-        return remote(src, part(term, u, d, s), term_send.at[d, lax.rem(s, 2), u], term_recv.at[d, s, u], partner)
+        return remote(src, part(term, u, d, s), term_send.at[units[u][0]], term_recv.at[d, lax.rem(s, 2), u], partner)
 
     def rs_copy(u, d, s):
-        return remote(part(term, u, d, s), part(run, u, d, s), rs_send.at[d, lax.rem(s, 2), u], rs_recv.at[d, s, u], ahead[d])
+        return remote(part(term, u, d, s), part(run, u, d, s), rs_send.at[units[u][0]], ring_recv.at[d, s, u], ahead[d])
 
     def ag_copy(u, d, t, block=None):
         at = part(w_out, u, d, 2 * (ag_block(d, t) if block is None else block) + core)
-        return remote(at, at, ag_send.at[d, lax.rem(t, 2), u], ag_recv.at[d, t, u], ahead[d])
+        return remote(at, at, ag_send.at[units[u][0]], ring_recv.at[d, lax.rem(chips - 1 + t, chips), u], ahead[d])
 
     def ag_arrival(u, d, t):
         return ag_copy(u, d, t, ag_block(d, t + 1))
 
     def fw_copy(u, d, t, whose):
         at = part(w_out, u, d, 2 * ag_block(d, t) + whose)
-        return remote(at, at, fw_send.at[d, lax.rem(t, 2), u], fw_recv.at[d, t, u], partner)
-
-    def mom_copies(u, d):
+        return remote(at, at, fw_send.at[units[u][0]], fw_recv.at[units[u][0]], partner)
+
+    def mom_copies(k):
         return (
-            pltpu.make_async_copy(part(m_in, u, d), part(m_out, u, d), mom_sem.at[0, d, u]),
-            pltpu.make_async_copy(part(v_in, u, d), part(v_out, u, d), mom_sem.at[1, d, u]),
-            pltpu.make_async_copy(part(w, u, d, me), part(w_out, u, d, me), mom_sem.at[2, d, u]),
+            pltpu.make_async_copy(m_in[k], m_out[k], mom_sem.at[0, k]),
+            pltpu.make_async_copy(v_in[k], v_out[k], mom_sem.at[1, k]),
+            pltpu.make_async_copy(w[k].at[:, me], w_out[k].at[:, me], mom_sem.at[2, k]),
         )
+
+    def all_of(k, blocks, send, recv):
+        at = w_out[k].at[0, pl.ds(0, blocks)]
+        return remote(at, at, send.at[k], recv.at[k], partner)
 
     for u, d in chunks:
         own_copy(u, d, 0).start()
@@ -130,21 +131,13 @@
 
             rows_loop(row, rows, mine.shape[1], add)
             own_copy(u, d, s + 1).start()
-            if not first:
-                term_copy(u, d, s - 1).wait_send()
+            rs_copy(u, d, s).start()
             term_copy(u, d, s + 1).start()
-            if not first:
-
-                @pl.when(s >= 2)
-                def _():
-                    rs_copy(u, d, s - 2).wait_send()
-
-            rs_copy(u, d, s).start()
-            if first:
-                for copy in mom_copies(u, d):
-                    copy.start()
 
     scatter_step(0, True)
+    for k in range(3):
+        for copy in mom_copies(k):
+            copy.start()
     lax.fori_loop(1, chips - 1, lambda s, c: (scatter_step(s, False), c)[1], 0)
 
     last = chips - 1
@@ -152,8 +145,9 @@
         k, row, rows = units[u]
         own_copy(u, d, last).wait()
         term_copy(u, d, last).wait_recv()
-        for copy in mom_copies(u, d):
-            copy.wait()
+        if d == 0 and row == 0:
+            for copy in mom_copies(k):
+                copy.wait()
         rs_copy(u, d, last - 1).wait_recv()
         mine, other, sums = own[k].at[d, last % 2], term[k].at[d, last], run[k].at[d, last - 1]
         mo, vo, wo = m_out[k].at[d], v_out[k].at[d], w_out[k].at[d, me]
@@ -167,21 +161,12 @@
             wo[at, :] = new_w
 
         rows_loop(row, rows, mine.shape[1], update)
-        term_copy(u, d, last - 1).wait_send()
-        term_copy(u, d, last).wait_send()
         ag_copy(u, d, 0).start()
         fw_copy(u, d, 0, core).start()
-        rs_copy(u, d, last - 2).wait_send()
 
     def gather_step(t, c):
         for u, d in chunks:
             ag_arrival(u, d, t - 1).wait_recv()
-
-            @pl.when(t >= 2)
-            def _():
-                ag_copy(u, d, t - 2).wait_send()
-                fw_copy(u, d, t - 2, core).wait_send()
-
             ag_copy(u, d, t).start()
             fw_copy(u, d, t, core).start()
         return c
@@ -189,21 +174,12 @@
     lax.fori_loop(1, chips - 1, gather_step, 0)
     for u, d in chunks:
         ag_arrival(u, d, last - 1).wait_recv()
-        fw_copy(u, d, last - 2, core).wait_send()
         fw_copy(u, d, last, core).start()
-    for u, d in chunks:
-        rs_copy(u, d, last - 1).wait_send()
-        ag_copy(u, d, last - 2).wait_send()
-        ag_copy(u, d, last - 1).wait_send()
-        fw_copy(u, d, last - 1, core).wait_send()
-        fw_copy(u, d, last, core).wait_send()
-
-    def landed(t, c):
-        for u, d in chunks:
-            fw_copy(u, d, t, 1 - core).wait_recv()
-        return c
-
-    lax.fori_loop(0, chips, landed, 0)
+    for k in range(3):
+        all_of(k, n, term_send, fw_recv).wait_send()
+        all_of(k, n - 2, rs_send, fw_recv).wait_send()
+        all_of(k, n - 2, ag_send, fw_recv).wait_send()
+        all_of(k, n, fw_send, fw_recv).wait()
 
 
 def write_out(*refs):
@@ -240,15 +216,14 @@
                 *(pltpu.VMEM((layers, chips, *b), BF16) for b in blocks),
                 *(pltpu.VMEM((layers, chips - 1, *b), BF16) for b in blocks),
                 dma((layers, 2, count)),
-                dma((3, layers, count)),
+                dma((3, 3)),
+                dma((3,)),
                 dma((layers, 2, count)),
+                dma((3,)),
+                dma((3,)),
                 dma((layers, chips, count)),
-                dma((layers, 2, count)),
-                dma((layers, chips - 1, count)),
-                dma((layers, 2, count)),
-                dma((layers, chips - 1, count)),
-                dma((layers, 2, count)),
-                dma((layers, chips, count)),
+                dma((3,)),
+                dma((3,)),
             ],
             compiler_params=pltpu.CompilerParams(collective_id=0, has_side_effects=True, vmem_limit_bytes=28 * 1024 * 1024),
         )(*terms, *weights, *m, *v)
@@ -257,7 +232,7 @@
             out_shape=[pltpu.HBM(o.shape, o.dtype) for o in part],
             in_specs=[pl.BlockSpec(memory_space=pltpu.VMEM)] * len(part),
             out_specs=[pl.BlockSpec(memory_space=pltpu.HBM)] * len(part),
-            scratch_shapes=[dma((9, layers))],
+            scratch_shapes=[dma((len(part), layers))],
             compiler_params=pltpu.CompilerParams(vmem_limit_bytes=1024 * 1024),
         )(*part) for part in (out[:3], out[3:])]
         out = [x for p in out for x in p]

time: 278 us -> 275 us (0.989)
  no operation moved by 1% of the time
where the time goes in v3:
time: 275 us
  Pallas kernels  275 us (100%)
    pallas_call x1, Pallas kernels, step(): pl.pallas_call(functools.partial(kernel, n), out_shape=[pltpu.VMEM((layer...  263 us
    pallas_call x2, Pallas kernels, step(): pl.pallas_call(write_out, out_shape=[pltpu.HBM(o.shape, o.dtype) for o in...  11.8 us

profile of v3, /device:TPU:21, one launch (start us, length us, event | category | flops | bytes accessed | tf_op | source)
XLA Modules:
  0.0 275.3 jit_solution(10404100780721442441)
XLA Ops:
  0.6 262.8 %shard_map.187 = (bf16[2,16,40,3456]{3,2,1,0:T(8,128)(2,1)S(1)}, bf16[2,16,40,3456]{3,2,1,0:T(8,128)(2,1)S(1)}, bf16[2,16,216,640]{3,2,1,0:T(8,128)(2,1)S(1)}, f...) custom-call(bf16[2,16,40,3456]{3,2,1,0:T(8,128)(2,1)} %bitcast.9, ...), custom_call_target="tpu_custom_call" | custom-call | tf_op jit(solution)/shard_map/pallas_call | solution.py:209
  263.5 8.9 %shard_map.188 = (bf16[2,16,40,3456]{3,2,1,0:T(8,128)(2,1)}, bf16[2,16,40,3456]{3,2,1,0:T(8,128)(2,1)}, bf16[2,16,216,640]{3,2,1,0:T(8,128)(2,1)}) custom-call(bf16[2,16,40,3456]{3,2,1,0:T(8,128)(2,1)S(1)} %get-tuple-element.27.refs_0_, bf16[2,16,40,3456]{3,2,1,0:T(8,128)(2,1)S(1)} %get-tuple-element.28.refs_1_, ...), custom_call_target="tpu_custom_call" | custom-call | tf_op jit(solution)/shard_map/pallas_call | solution.py:230
  272.4 2.9 %shard_map.189 = (f32[2,40,3456]{2,1,0:T(8,128)}, f32[2,40,3456]{2,1,0:T(8,128)}, f32[2,216,640]{2,1,0:T(8,128)}, f32[2,40,3456]{2,1,0:T(8,128)}, f32[2,40,3456]{2,1,0:T(8,128)}, /*index=5*/f32[2,216,640]{2,1,0:T(8,128)}) custom-call(f32[2,40,3456]{2,1,0:T(8,128)S(1)} %get-tuple-element.33.refs_0_, f32[2,40,3456]{2,1,0:T(8,128)S(1)} %get-tuple-element.34.refs_1_, ...), custom_call_target="tpu_custom_call" | custom-call | tf_op jit(solution)/shard_map/pallas_call | solution.py:230

commit v4 on v3

v4 whole, which is shorter than its diff:
```python
import functools

import jax
import jax.numpy as jnp
from jax import lax
from jax.experimental import pallas as pl
from jax.experimental.pallas import tpu as pltpu
from jax.sharding import PartitionSpec as P

MESH = pl.DeviceIdType.MESH
F32 = jnp.float32
BF16 = jnp.bfloat16
TILE = 8
EARLY = 5
JOIN = 5
CUTS = 7


def adamw(w, m, v, g):
    m = 0.9 * m + 0.1 * g
    v = 0.95 * v + 0.05 * g * g
    step = m * lax.rsqrt(v + 1e-8) + 0.1 * w
    return (w - 0.02 * step).astype(BF16), m, v


def pieces_of(blocks):
    whole = [(k, 0, b[0], k) for k, b in enumerate(blocks)]
    top = blocks[0][0]
    return whole, [(0, 0, TILE, len(blocks)), (0, TILE, top - TILE, 0), *whole[1:]]


def thirds_of(rows):
    tiles = rows // TILE
    count = min(CUTS, tiles)
    cuts = [TILE * (tiles * i // count) for i in range(count + 1)]
    return [(a, b - a) for a, b in zip(cuts, cuts[1:])]


def rows_loop(first, rows, cols, body):
    step = TILE
    while rows % (2 * step) == 0 and 2 * step * cols <= 32 * 1024:
        step *= 2
    while rows % (3 * step) == 0 and 3 * step * cols <= 32 * 1024:
        step *= 3

    def one(i, carry):
        body(pl.ds(pl.multiple_of(first + i * step, TILE), step))
        return carry

    lax.fori_loop(0, rows // step, one, 0)


def kernel(n, *refs):
    g, w, m_in, v_in, w_out, m_out, v_out = (refs[i : i + 3] for i in range(0, 21, 3))
    own, term, run = (refs[i : i + 3] for i in range(21, 30, 3))
    stage, stage_sem, own_sem, own_short, mom_sem, term_recv, term_short, ring_recv, ring_send, chip_send, fw_recv, down_recv, down_send = refs[30:]
    chips = n // 2
    last = chips - 1
    me = lax.axis_index("dp")
    z, core = me // 2, lax.rem(me, 2)
    partner = me + 1 - 2 * core
    sign = (1, -1)
    ahead = [lax.rem(me + 2 * sign[d] + n, n) for d in range(2)]
    whole, head = pieces_of([one.shape[1:] for one in m_in])
    most, thirds = whole[:-1], thirds_of(whole[-1][2])

    def both(pieces):
        return [(p, d) for p in pieces for d in range(2)]

    def part(refs, p, *at):
        return refs[p[0]].at[(*at, pl.ds(p[1], p[2]))]

    def sem(many, short, p, d, slot):
        return short.at[d] if p[3] == len(whole) else many.at[d, slot, p[3]]

    def rs_block(d, s):
        return lax.rem(z - sign[d] * (s + 1) + 2 * chips, chips)

    def ag_block(d, t):
        return lax.rem(z - sign[d] * t + chips, chips)

    def remote(src, dst, send, recv, to):
        return pltpu.make_async_remote_copy(src_ref=src, dst_ref=dst, send_sem=send, recv_sem=recv, device_id={"dp": to}, device_id_type=MESH)

    def own_copy(p, d, s):
        slot = lax.rem(s, 2)
        return pltpu.make_async_copy(part(g, p, d, 2 * rs_block(d, s) + core), part(own, p, d, slot), sem(own_sem, own_short, p, d, slot))

    def stage_copy(p, d):
        return pltpu.make_async_copy(part(g, p, d, 2 * rs_block(d, 0) + 1 - core), stage.at[d], stage_sem.at[d])

    def term_copy(p, d, s, src=None):
        src = part(g, p, d, 2 * rs_block(d, s) + 1 - core) if src is None else src
        return remote(src, part(term, p, d, s), chip_send.at[p[0]], sem(term_recv, term_short, p, d, lax.rem(s, 2)), partner)

    def rs_copy(p, d, s):
        return remote(part(term, p, d, s), part(run, p, d, s), ring_send.at[p[0]], ring_recv.at[d, lax.rem(s, 3), p[0]], ahead[d])

    def ag_copy(p, d, t, block=None):
        at = part(w_out, p, d, 2 * (ag_block(d, t) if block is None else block) + core)
        return remote(at, at, ring_send.at[p[0]], ring_recv.at[d, lax.rem(last + t, 3), p[0]], ahead[d])

    def ag_arrival(p, d, t):
        return ag_copy(p, d, t, ag_block(d, t + 1))

    def fw_copy(p, d, t):
        at = part(w_out, p, d, 2 * ag_block(d, t) + core)
        return remote(at, at, chip_send.at[p[0]], fw_recv.at[p[0]], partner)

    def mom_copies(k):
        return (
            pltpu.make_async_copy(m_in[k], m_out[k], mom_sem.at[k]),
            pltpu.make_async_copy(v_in[k], v_out[k], mom_sem.at[k]),
            pltpu.make_async_copy(w[k].at[:, me], w_out[k].at[:, me], mom_sem.at[k]),
        )

    def bytes_of(at, semaphore):
        return pltpu.make_async_copy(at, at, semaphore)

    barrier = pltpu.get_barrier_semaphore()
    for peer in (partner, *ahead):
        pl.semaphore_signal(barrier, inc=1, device_id={"dp": peer}, device_id_type=MESH)
    for p, d in both(head[:1]):
        stage_copy(p, d).start()
    for p, d in both(head):
        own_copy(p, d, 0).start()
    pl.semaphore_wait(barrier, 3)

    for p, d in both(head):
        if p is head[0]:
            stage_copy(p, d).wait()
            term_copy(p, d, 0, stage.at[d]).start()
        else:
            term_copy(p, d, 0).start()

    def scatter_step(s, pieces, first):
        for p, d in both(pieces):
            k, row, rows, _ = p
            own_copy(p, d, s).wait()
            term_copy(p, d, s).wait_recv()
            if not first:
                rs_copy(p, d, s - 1).wait_recv()
            mine, other, sums = own[k].at[d, lax.rem(s, 2)], term[k].at[d, s], run[k].at[d, s - 1]

            def add(at):
                total = mine[at, :].astype(F32) + other[at, :].astype(F32)
                if not first:
                    total += sums[at, :].astype(F32)
                other[at, :] = total.astype(BF16)

            rows_loop(row, rows, mine.shape[1], add)
            if p[3] < len(whole):
                own_copy(whole[k], d, s + 1).start()
            rs_copy(p, d, s).start()
            if p[3] < len(whole):
                term_copy(whole[k], d, s + 1).start()

    scatter_step(0, head, True)
    for k in range(3):
        for copy in mom_copies(k):
            copy.start()
    lax.fori_loop(1, last, lambda s, c: (scatter_step(s, whole, False), c)[1], 0)

    for p, d in both(whole):
        k, row, rows, _ = p
        own_copy(p, d, last).wait()
        term_copy(p, d, last).wait_recv()
        if d == 0:
            bytes_of(w_out[k].at[0, pl.ds(0, 5 * m_in[k].shape[0])], mom_sem.at[k]).wait()
        rs_copy(p, d, last - 1).wait_recv()
        mine, other, sums = own[k].at[d, last % 2], term[k].at[d, last], run[k].at[d, last - 1]
        mo, vo, wo = m_out[k].at[d], v_out[k].at[d], w_out[k].at[d, me]

        def update(at):
            total = mine[at, :].astype(F32) + other[at, :].astype(F32) + sums[at, :].astype(F32)
            grad = total.astype(BF16).astype(F32)
            new_w, new_m, new_v = adamw(wo[at, :].astype(F32), mo[at, :], vo[at, :], grad)
            wo[at, :] = new_w
            mo[at, :] = new_m
            vo[at, :] = new_v

        rows_loop(row, rows, mine.shape[1], update)
        if p in most:
            ag_copy(p, d, 0).start()
            fw_copy(p, d, 0).start()

    def gather_step(t, c):
        for p, d in both(most):
            ag_arrival(p, d, t - 1).wait_recv()
            ag_copy(p, d, t).start()
            fw_copy(p, d, t).start()
        return c

    lax.fori_loop(1, last, gather_step, 0)
    for p, d in both(most):
        ag_arrival(p, d, last - 1).wait_recv()
        fw_copy(p, d, last).start()

    def down_copy(p, d, t, block):
        at = w_out[-1].at[d, 2 * block + core, pl.ds(p[0], p[1])]
        return remote(at, at, down_send, down_recv.at[d, lax.rem(t, 3), thirds.index(p)], ahead[d])

    @pl.when(core == 1)
    def _():
        for p, d in both(thirds):
            down_copy(p, d, 0, ag_block(d, 0)).start()

        def early_step(t, c):
            for p, d in both(thirds):
                down_copy(p, d, t - 1, ag_block(d, t)).wait_recv()
                down_copy(p, d, t, ag_block(d, t)).start()
            return c

        lax.fori_loop(1, EARLY, early_step, 0)
        for p, d in both(thirds):
            down_copy(p, d, EARLY - 1, ag_block(d, EARLY)).wait_recv()
        bytes_of(w_out[-1].at[0, pl.ds(0, 2 * EARLY)], down_send).wait()

    for k in range(3):
        if k < 2:
            bytes_of(w_out[k].at[:, pl.ds(0, n - 2)], ring_send.at[k]).wait()
            bytes_of(w_out[k], chip_send.at[k]).wait()
            bytes_of(w_out[k].at[0], fw_recv.at[k]).wait()
        else:
            bytes_of(w_out[k].at[0, pl.ds(0, n - 2)], ring_send.at[k]).wait()
            bytes_of(w_out[k].at[0], chip_send.at[k]).wait()


def rest_kernel(n, held, after, rest, ready, ring_send, ring_recv, chip_send, chip_recv):
    chips = n // 2
    last = chips - 1
    me = lax.axis_index("dp")
    z, core = me // 2, lax.rem(me, 2)
    partner = me + 1 - 2 * core
    sign = (1, -1)
    ahead = [lax.rem(me + 2 * sign[d] + n, n) for d in range(2)]
    thirds = thirds_of(held.shape[2])
    pieces = [(p, d) for p in thirds for d in range(2)]
    had = core * EARLY
    join = jnp.where(core == 0, JOIN, EARLY + 1)

    barrier = pltpu.get_barrier_semaphore()
    for peer in ahead:
        pl.semaphore_signal(barrier, inc=1, device_id={"dp": peer}, device_id_type=MESH)

    @pl.when(core == 0)
    def _():
        pl.semaphore_signal(barrier, inc=1, device_id={"dp": partner}, device_id_type=MESH)

    pl.semaphore_wait(barrier, 2 + core)

    @pl.when(core == 1)
    def _():
        pl.semaphore_signal(ready, inc=1, device_id={"dp": partner}, device_id_type=MESH)

    def at(ref, p, d, t):
        return ref.at[d, 2 * lax.rem(z - sign[d] * t + chips, chips) + core, pl.ds(p[0], p[1])]

    def remote(src, dst, send, recv, to):
        return pltpu.make_async_remote_copy(src_ref=src, dst_ref=dst, send_sem=send, recv_sem=recv, device_id={"dp": to}, device_id_type=MESH)

    def ring_copy(src, p, d, t):
        return remote(at(src, p, d, t), at(rest, p, d, t), ring_send, ring_recv.at[d, lax.rem(t, 3), thirds.index(p)], ahead[d])

    def arrive(p, d, t):
        there = at(rest, p, d, t)
        remote(there, there, ring_send, ring_recv.at[d, lax.rem(t - 1, 3), thirds.index(p)], ahead[d]).wait_recv()

    def fw_copy(src, p, d, t):
        return remote(at(src, p, d, t), at(rest, p, d, t), chip_send, chip_recv, partner)

    for p, d in pieces:
        ring_copy(held, p, d, had).start()

    def step(t, c, forward):
        for p, d in pieces:
            arrive(p, d, t)
            ring_copy(rest, p, d, t).start()
            if forward:
                fw_copy(rest, p, d, t).start()
        return c

    def catch_up(src):
        def one(t, c):
            for p, d in pieces:
                fw_copy(src, p, d, t).start()
            return c

        return one

    lax.fori_loop(had + 1, join, functools.partial(step, forward=False), 0)

    @pl.when(core == 0)
    def _():
        pl.semaphore_wait(ready, 1)

    lax.fori_loop(0, had + 1, catch_up(held), 0)
    lax.fori_loop(had + 1, join, catch_up(rest), 0)
    lax.fori_loop(join, last, functools.partial(step, forward=True), 0)
    for p, d in pieces:
        arrive(p, d, last)
        fw_copy(rest, p, d, last).start()

    for which, count in enumerate((2 * last, 2 * (last - EARLY))):

        @pl.when(core == which)
        def _():
            part = rest.at[0, pl.ds(0, count)]
            pltpu.make_async_copy(part, part, ring_send).wait()

    pltpu.make_async_copy(rest.at[0], rest.at[0], chip_send).wait()
    pltpu.make_async_copy(rest.at[0], rest.at[0], chip_recv).wait()


def write_rest(n, held, rest, out, sem):
    chips = n // 2
    me = lax.axis_index("dp")
    z, core = me // 2, lax.rem(me, 2)
    for d, sign in ((0, 1), (1, -1)):
        for t in range(chips):
            block = 2 * lax.rem(z - sign * t + chips, chips) + core
            in_held = t <= core * EARLY
            for src, cond in ((held, in_held), (rest, jnp.logical_not(in_held))):

                @pl.when(cond)
                def _():
                    pltpu.make_async_copy(src.at[d, block], out.at[d, block], sem).start()

            other = 2 * t + 1 - core
            pltpu.make_async_copy(rest.at[d, other], out.at[d, other], sem).start()
    pltpu.make_async_copy(rest, rest, sem).wait()


def write_out(*refs):
    count = len(refs) // 2 - 1
    mark, sem = refs[-2:]
    copies = []
    for i in range(count):
        for j in range(refs[i].shape[0]):
            copies.append(pltpu.make_async_copy(refs[i].at[j], refs[count + i].at[j], sem.at[i, j]))
    for copy in copies:
        copy.start()
    mark[...] = jnp.zeros_like(mark)
    for copy in copies:
        copy.wait()


def solution(mesh):
    n = mesh.shape["dp"]
    chips = n // 2

    def step(*arrays):
        terms, weights, m, v = (arrays[i : i + 3] for i in (0, 3, 6, 9))
        layers = m[0].shape[0]
        blocks = [(one.shape[1], one.shape[2]) for one in m]
        terms = [t.reshape(layers, n, *b) for t, b in zip(terms, blocks, strict=True)]
        weights = [w.reshape(layers, n, *b) for w, b in zip(weights, blocks, strict=True)]
        dma = pltpu.SemaphoreType.DMA
        thirds = thirds_of(blocks[-1][0])
        out = pl.pallas_call(
            functools.partial(kernel, n),
            out_shape=[pltpu.VMEM((layers, n, *b), BF16) for b in blocks] + [pltpu.VMEM((layers, *b), F32) for b in blocks] * 2,
            in_specs=[pl.BlockSpec(memory_space=pltpu.HBM)] * 12,
            out_specs=[pl.BlockSpec(memory_space=pltpu.VMEM)] * 9,
            scratch_shapes=[
                *(pltpu.VMEM((layers, 2, *b), BF16) for b in blocks),
                *(pltpu.VMEM((layers, chips, *b), BF16) for b in blocks),
                *(pltpu.VMEM((layers, chips - 1, *b), BF16) for b in blocks),
                pltpu.VMEM((layers, TILE, blocks[0][1]), BF16),
                dma((layers,)),
                dma((layers, 2, 3)),
                dma((layers,)),
                dma((3,)),
                dma((layers, 2, 3)),
                dma((layers,)),
                dma((layers, 3, 3)),
                dma((3,)),
                dma((3,)),
                dma((3,)),
                dma((layers, 3, len(thirds))),
                dma,
            ],
            compiler_params=pltpu.CompilerParams(collective_id=0, has_side_effects=True, vmem_limit_bytes=28 * 1024 * 1024),
        )(*terms, *weights, *m, *v)
        held, ready = out[2], [*out[:2], *out[3:]]
        *done, mark = pl.pallas_call(
            write_out,
            out_shape=[*(pltpu.HBM(o.shape, o.dtype) for o in ready), jax.ShapeDtypeStruct((TILE, 128), F32)],
            in_specs=[pl.BlockSpec(memory_space=pltpu.VMEM)] * len(ready),
            out_specs=[pl.BlockSpec(memory_space=pltpu.HBM)] * len(ready) + [pl.BlockSpec(memory_space=pltpu.VMEM)],
            scratch_shapes=[dma((len(ready), layers))],
            compiler_params=pltpu.CompilerParams(vmem_limit_bytes=1024 * 1024),
        )(*ready)
        rest = pl.pallas_call(
            functools.partial(rest_kernel, n),
            out_shape=pltpu.VMEM(held.shape, held.dtype),
            in_specs=[pl.BlockSpec(memory_space=pltpu.VMEM)] * 2,
            out_specs=pl.BlockSpec(memory_space=pltpu.VMEM),
            scratch_shapes=[pltpu.SemaphoreType.REGULAR, dma, dma((layers, 3, len(thirds))), dma, dma],
            compiler_params=pltpu.CompilerParams(collective_id=1, has_side_effects=True, vmem_limit_bytes=1024 * 1024),
        )(held, mark)
        down = pl.pallas_call(
            functools.partial(write_rest, n),
            out_shape=pltpu.HBM(held.shape, held.dtype),
            in_specs=[pl.BlockSpec(memory_space=pltpu.VMEM)] * 2,
            out_specs=pl.BlockSpec(memory_space=pltpu.HBM),
            scratch_shapes=[dma],
            compiler_params=pltpu.CompilerParams(vmem_limit_bytes=1024 * 1024),
        )(held, rest)
        out = [*done[:2], down, *done[2:]]
        whole = [one.reshape(layers, n * b[0], b[1]) for one, b in zip(out[:3], blocks, strict=True)]
        return (*whole, *out[3:])

    all_of, cut = P(None, None, None), P(None, "dp", None)
    return jax.shard_map(
        step,
        mesh=mesh,
        in_specs=(P(("rep", "dp"), None, None, None),) * 3 + (all_of,) * 3 + (cut,) * 6,
        out_specs=(P("rep", None, None),) * 3 + (P("rep", "dp", None),) * 6,
        check_vma=False,
    )
```

time: 275 us -> 270 us (0.982)
  Pallas kernels: 275 us -> 269 us
    pallas_call x1, Pallas kernels: 263 us -> 239 us  [step(): pl.pallas_call(functools.partial(kernel, n), out_shape=[pltpu.VMEM((layer...]
    pallas_call x2 -> x3, Pallas kernels: 11.8 us -> 30 us  [the longest x1 18.3 us: step(): pl.pallas_call(functools.partial(rest_kernel, n), out_shape=pltpu.VMEM(he...]
where the time goes in v4:
time: 270 us
  Pallas kernels  269 us (100%)
    pallas_call x1, Pallas kernels, step(): pl.pallas_call(functools.partial(kernel, n), out_shape=[pltpu.VMEM((layer...  239 us
    pallas_call x1, Pallas kernels, step(): pl.pallas_call(functools.partial(rest_kernel, n), out_shape=pltpu.VMEM(he...  18.3 us
    pallas_call x1, Pallas kernels, step(): pl.pallas_call(write_out, out_shape=[*(pltpu.HBM(o.shape, o.dtype) for o...  8.22 us

profile of v4, /device:TPU:21, one launch (start us, length us, event | category | flops | bytes accessed | tf_op | source)
XLA Modules:
  0.0 270.0 jit_solution(11418573583334799001)
XLA Ops:
  0.6 239.3 %shard_map.187 = (bf16[2,16,40,3456]{3,2,1,0:T(8,128)(2,1)S(1)}, bf16[2,16,40,3456]{3,2,1,0:T(8,128)(2,1)S(1)}, bf16[2,16,216,640]{3,2,1,0:T(8,128)(2,1)S(1)}, f...) custom-call(bf16[2,16,40,3456]{3,2,1,0:T(8,128)(2,1)} %bitcast.9, ...), custom_call_target="tpu_custom_call" | custom-call | tf_op jit(solution)/shard_map/pallas_call | solution.py:360
  240.0 8.2 %shard_map.188 = (bf16[2,16,40,3456]{3,2,1,0:T(8,128)(2,1)}, bf16[2,16,40,3456]{3,2,1,0:T(8,128)(2,1)}, f32[2,40,3456]{2,1,0:T(8,128)}, f32[2,40,3456]{2,1,0:T(8...) custom-call(bf16[2,16,40,3456]{3,2,1,0:T(8,128)(2,1)S(1)} %get-tuple, ...), custom_call_target="tpu_custom_call" | custom-call | tf_op jit(solution)/shard_map/pallas_call | solution.py:386
  248.2 18.3 %shard_map.189.rest = bf16[2,16,216,640]{3,2,1,0:T(8,128)(2,1)S(1)} custom-call(bf16[2,16,216,640]{3,2,1,0:T(8,128)(2,1)S(1)} %get-tuple-element.37.held, f32[8,128]{1,0:T(8,128)S(1)} %get-tuple-element.38.after), custom_call_target="tpu_custom_call" | custom-call | tf_op jit(solution)/shard_map/pallas_call | solution.py:394
  266.5 3.4 %shard_map.190 = bf16[2,16,216,640]{3,2,1,0:T(8,128)(2,1)} custom-call(bf16[2,16,216,640]{3,2,1,0:T(8,128)(2,1)S(1)} %get-tuple-element.37.held, bf16[2,16,216,640]{3,2,1,0:T(8,128)(2,1)S(1)} %shard_map.189.rest), custom_call_target="tpu_custom_call" | custom-call | tf_op jit(solution)/shard_map/pallas_call | solution.py:402

commit v5 on v4

--- a/solution.py
+++ b/solution.py
@@ -11,8 +11,8 @@
 F32 = jnp.float32
 BF16 = jnp.bfloat16
 TILE = 8
-EARLY = 5
-JOIN = 5
+EARLY = 6
+JOIN = 6
 CUTS = 7
 
 
@@ -192,10 +192,6 @@
         return c
 
     lax.fori_loop(1, last, gather_step, 0)
-    for p, d in both(most):
-        ag_arrival(p, d, last - 1).wait_recv()
-        fw_copy(p, d, last).start()
-
     def down_copy(p, d, t, block):
         at = w_out[-1].at[d, 2 * block + core, pl.ds(p[0], p[1])]
         return remote(at, at, down_send, down_recv.at[d, lax.rem(t, 3), thirds.index(p)], ahead[d])
@@ -205,6 +201,12 @@
         for p, d in both(thirds):
             down_copy(p, d, 0, ag_block(d, 0)).start()
 
+    for p, d in both(most):
+        ag_arrival(p, d, last - 1).wait_recv()
+        fw_copy(p, d, last).start()
+
+    @pl.when(core == 1)
+    def _():
         def early_step(t, c):
             for p, d in both(thirds):
                 down_copy(p, d, t - 1, ag_block(d, t)).wait_recv()
@@ -282,8 +284,8 @@
 
     def catch_up(src):
         def one(t, c):
-            for p, d in pieces:
-                fw_copy(src, p, d, t).start()
+            for d in range(2):
+                fw_copy(src, (0, held.shape[2]), d, t).start()
             return c
 
         return one

time: 270 us -> 268 us (level)
    pallas_call x1, Pallas kernels: 18.3 us -> 15.3 us  [step(): pl.pallas_call(functools.partial(rest_kernel, n), out_shape=pltpu.VMEM(he...]
where the time goes in v5:
time: 268 us
  Pallas kernels  267 us (100%)
    pallas_call x1, Pallas kernels, step(): pl.pallas_call(functools.partial(kernel, n), out_shape=[pltpu.VMEM((layer...  240 us
    pallas_call x1, Pallas kernels, step(): pl.pallas_call(functools.partial(rest_kernel, n), out_shape=pltpu.VMEM(he...  15.3 us
    pallas_call x1, Pallas kernels, step(): pl.pallas_call(write_out, out_shape=[*(pltpu.HBM(o.shape, o.dtype) for o...  8.22 us

profile of v5, /device:TPU:21, one launch (start us, length us, event | category | flops | bytes accessed | tf_op | source)
XLA Modules:
  0.0 267.6 jit_solution(14028260552910576708)
XLA Ops:
  0.6 240.0 %shard_map.187 = (bf16[2,16,40,3456]{3,2,1,0:T(8,128)(2,1)S(1)}, bf16[2,16,40,3456]{3,2,1,0:T(8,128)(2,1)S(1)}, bf16[2,16,216,640]{3,2,1,0:T(8,128)(2,1)S(1)}, f...) custom-call(bf16[2,16,40,3456]{3,2,1,0:T(8,128)(2,1)} %bitcast.9, ...), custom_call_target="tpu_custom_call" | custom-call | tf_op jit(solution)/shard_map/pallas_call | solution.py:362
  240.6 8.2 %shard_map.188 = (bf16[2,16,40,3456]{3,2,1,0:T(8,128)(2,1)}, bf16[2,16,40,3456]{3,2,1,0:T(8,128)(2,1)}, f32[2,40,3456]{2,1,0:T(8,128)}, f32[2,40,3456]{2,1,0:T(8...) custom-call(bf16[2,16,40,3456]{3,2,1,0:T(8,128)(2,1)S(1)} %get-tuple, ...), custom_call_target="tpu_custom_call" | custom-call | tf_op jit(solution)/shard_map/pallas_call | solution.py:388
  248.8 15.3 %shard_map.189.rest = bf16[2,16,216,640]{3,2,1,0:T(8,128)(2,1)S(1)} custom-call(bf16[2,16,216,640]{3,2,1,0:T(8,128)(2,1)S(1)} %get-tuple-element.37.held, f32[8,128]{1,0:T(8,128)S(1)} %get-tuple-element.38.after), custom_call_target="tpu_custom_call" | custom-call | tf_op jit(solution)/shard_map/pallas_call | solution.py:396
  264.2 3.4 %shard_map.190 = bf16[2,16,216,640]{3,2,1,0:T(8,128)(2,1)} custom-call(bf16[2,16,216,640]{3,2,1,0:T(8,128)(2,1)S(1)} %get-tuple-element.37.held, bf16[2,16,216,640]{3,2,1,0:T(8,128)(2,1)S(1)} %shard_map.189.rest), custom_call_target="tpu_custom_call" | custom-call | tf_op jit(solution)/shard_map/pallas_call | solution.py:404

commit v6 on v5

--- a/solution.py
+++ b/solution.py
@@ -13,7 +13,8 @@
 TILE = 8
 EARLY = 6
 JOIN = 6
-CUTS = 7
+CUTS = 9
+CUTS_EARLY = 3
 
 
 def adamw(w, m, v, g):
@@ -29,9 +30,9 @@
     return whole, [(0, 0, TILE, len(blocks)), (0, TILE, top - TILE, 0), *whole[1:]]
 
 
-def thirds_of(rows):
+def thirds_of(rows, cuts=None):
     tiles = rows // TILE
-    count = min(CUTS, tiles)
+    count = min(cuts or CUTS, tiles)
     cuts = [TILE * (tiles * i // count) for i in range(count + 1)]
     return [(a, b - a) for a, b in zip(cuts, cuts[1:])]
 
@@ -62,7 +63,7 @@
     sign = (1, -1)
     ahead = [lax.rem(me + 2 * sign[d] + n, n) for d in range(2)]
     whole, head = pieces_of([one.shape[1:] for one in m_in])
-    most, thirds = whole[:-1], thirds_of(whole[-1][2])
+    most, thirds = whole[:-1], thirds_of(whole[-1][2], CUTS_EARLY)
 
     def both(pieces):
         return [(p, d) for p in pieces for d in range(2)]
@@ -358,7 +359,7 @@
         terms = [t.reshape(layers, n, *b) for t, b in zip(terms, blocks, strict=True)]
         weights = [w.reshape(layers, n, *b) for w, b in zip(weights, blocks, strict=True)]
         dma = pltpu.SemaphoreType.DMA
-        thirds = thirds_of(blocks[-1][0])
+        early, thirds = (thirds_of(blocks[-1][0], cuts) for cuts in (CUTS_EARLY, CUTS))
         out = pl.pallas_call(
             functools.partial(kernel, n),
             out_shape=[pltpu.VMEM((layers, n, *b), BF16) for b in blocks] + [pltpu.VMEM((layers, *b), F32) for b in blocks] * 2,
@@ -379,7 +380,7 @@
                 dma((3,)),
                 dma((3,)),
                 dma((3,)),
-                dma((layers, 3, len(thirds))),
+                dma((layers, 3, len(early))),
                 dma,
             ],
             compiler_params=pltpu.CompilerParams(collective_id=0, has_side_effects=True, vmem_limit_bytes=28 * 1024 * 1024),

time: 268 us -> 268 us (level)
  no operation moved by 1% of the time
where the time goes in v6:
time: 268 us
  Pallas kernels  267 us (100%)
    pallas_call x1, Pallas kernels, step(): pl.pallas_call(functools.partial(kernel, n), out_shape=[pltpu.VMEM((layer...  240 us
    pallas_call x1, Pallas kernels, step(): pl.pallas_call(functools.partial(rest_kernel, n), out_shape=pltpu.VMEM(he...  15.3 us
    pallas_call x1, Pallas kernels, step(): pl.pallas_call(write_out, out_shape=[*(pltpu.HBM(o.shape, o.dtype) for o...  8.22 us

profile of v6, /device:TPU:21, one launch (start us, length us, event | category | flops | bytes accessed | tf_op | source)
XLA Modules:
  0.0 267.6 jit_solution(4325223954144829651)
XLA Ops:
  0.6 240.0 %shard_map.187 = (bf16[2,16,40,3456]{3,2,1,0:T(8,128)(2,1)S(1)}, bf16[2,16,40,3456]{3,2,1,0:T(8,128)(2,1)S(1)}, bf16[2,16,216,640]{3,2,1,0:T(8,128)(2,1)S(1)}, f...) custom-call(bf16[2,16,40,3456]{3,2,1,0:T(8,128)(2,1)} %bitcast.9, ...), custom_call_target="tpu_custom_call" | custom-call | tf_op jit(solution)/shard_map/pallas_call | solution.py:363
  240.7 8.2 %shard_map.188 = (bf16[2,16,40,3456]{3,2,1,0:T(8,128)(2,1)}, bf16[2,16,40,3456]{3,2,1,0:T(8,128)(2,1)}, f32[2,40,3456]{2,1,0:T(8,128)}, f32[2,40,3456]{2,1,0:T(8...) custom-call(bf16[2,16,40,3456]{3,2,1,0:T(8,128)(2,1)S(1)} %get-tuple, ...), custom_call_target="tpu_custom_call" | custom-call | tf_op jit(solution)/shard_map/pallas_call | solution.py:389
  248.9 15.3 %shard_map.189.rest = bf16[2,16,216,640]{3,2,1,0:T(8,128)(2,1)S(1)} custom-call(bf16[2,16,216,640]{3,2,1,0:T(8,128)(2,1)S(1)} %get-tuple-element.37.held, f32[8,128]{1,0:T(8,128)S(1)} %get-tuple-element.38.after), custom_call_target="tpu_custom_call" | custom-call | tf_op jit(solution)/shard_map/pallas_call | solution.py:397
  264.2 3.4 %shard_map.190 = bf16[2,16,216,640]{3,2,1,0:T(8,128)(2,1)} custom-call(bf16[2,16,216,640]{3,2,1,0:T(8,128)(2,1)S(1)} %get-tuple-element.37.held, bf16[2,16,216,640]{3,2,1,0:T(8,128)(2,1)S(1)} %shard_map.189.rest), custom_call_target="tpu_custom_call" | custom-call | tf_op jit(solution)/shard_map/pallas_call | solution.py:405
